TPU v7x, 32 devices: a whole 2x2x4 slice. The times are simulated.
32 devices in a mesh: pool: 2 (over x), dp: 4 (over z), mp: 4 (over y, core).
Axes of the slice: x: 2, y: 2, z: 4, core: 2. Of those that a mesh axis runs over, the one named last changes fastest.
Arguments:
- states: bfloat16 [2, 4, 512, 8192], P('pool', 'dp', 'mp'), may hold values from -8 to 8
- lengths: int32 [2, 4], P(None, 'dp'), may hold values from 128 to 512
- gain: bfloat16 [2, 8192], replicated, may hold values from 0.099609375 to 1.8984375
- w_query: bfloat16 [2, 8192, 4096], P('pool', ('dp', 'mp')), may hold values from -0.088388348 to 0.088388348
- w_keyval: bfloat16 [2, 8192, 1024], P('pool', ('dp', 'mp')), may hold values from -0.088388348 to 0.088388348
Outputs:
- attended: bfloat16 [2, 4, 512, 4096], P('pool', 'dp', None, 'mp')
Inputs may be any that keep to these rules, and one draw needn't show every extreme that they name: `lengths`: live positions of each rollout; positions from it on are padding.
All inputs are finite; a program needn't handle non-finite values.
Results may differ from a plain program's by a relative error of at most 0.011.
Values may be sent and summed in bfloat16 or wider, within the bound.
No kernel may reach another device: no remote copies, remote signals or barrier semaphores. Data moves between devices by JAX's collectives and lax.ppermute only.
A program may use at most 128 MiB of HBM per device.

v0:
```python
import math
import jax
import jax.numpy as jnp
from jax import lax
from jax.sharding import PartitionSpec as P

HD = 128
QH = 32
KVH = 4


def partner(value, axis, distance):
    return lax.ppermute(value, axis, [(i, i ^ 1 << distance) for i in range(lax.axis_size(axis))])


def normalize(rows, gain_row):
    values = rows.astype(jnp.float32)
    meansq = jnp.mean(values * values, axis=-1, keepdims=True)
    return (values * lax.rsqrt(meansq + 1e-05) * gain_row.astype(jnp.float32)).astype(jnp.bfloat16)


def attend(query, keyval, length):
    seqlen = query.shape[0]
    local_heads = keyval.shape[1] // (2 * HD)
    groups = QH // KVH
    block = min(seqlen, 512)
    paired = keyval.reshape(seqlen, local_heads, 2 * HD)
    keys = paired[:, :, :HD]
    values = paired[:, :, HD:]
    places = jnp.arange(seqlen, dtype=jnp.int32)

    def one_block(index):
        start = index * block
        rows = query.reshape(block, local_heads, groups, HD)
        scores = jnp.einsum(
            "tkgd,skd->kgts", rows, keys, preferred_element_type=jnp.float32
        ) / math.sqrt(HD)
        qplaces = start + jnp.arange(block, dtype=jnp.int32)
        allowed = (places[None, :] <= qplaces[:, None]) & (places[None, :] < length)
        scores = jnp.where(allowed, scores, jnp.float32(-1e30))
        peak = jnp.max(scores, axis=-1, keepdims=True)
        expo = jnp.exp(scores - peak)
        probs = (expo / jnp.sum(expo, axis=-1, keepdims=True)).astype(jnp.bfloat16)
        result = jnp.einsum("kgts,skd->tkgd", probs, values, preferred_element_type=jnp.float32)
        result = result * (qplaces < length).astype(jnp.float32)[:, None, None, None]
        return result.reshape(block, local_heads * groups * HD).astype(jnp.bfloat16)

    blocks = lax.map(one_block, jnp.arange(seqlen // block, dtype=jnp.int32))
    return blocks.reshape(seqlen, local_heads * groups * HD)


def on_device(states, lengths, gain, w_query, w_keyval):
    own = lax.axis_index("pool")
    other = 1 - own
    normed = normalize(states, lax.dynamic_index_in_dim(gain, own, 0, keepdims=False))
    local_rows = lax.all_gather(normed, "mp", axis=2, tiled=True)
    whole = partner(local_rows, "pool", 0)
    rollouts = whole.shape[1]
    seqlen = whole.shape[2]
    tokens = whole[0].reshape(rollouts * seqlen, whole.shape[3])
    rows_query, rows_keyval = partner((w_query, w_keyval), "pool", 0)
    query_cols, keyval_cols = (
        lax.all_to_all(rows_query, "mp", split_axis=2, concat_axis=1, tiled=True),
        lax.all_to_all(rows_keyval, "mp", split_axis=2, concat_axis=1, tiled=True),
    )
    width_query = query_cols.shape[2]
    width_keyval = keyval_cols.shape[2]
    full_query, full_keyval = (
        lax.all_gather(query_cols, "dp", axis=1, tiled=True),
        lax.all_gather(keyval_cols, "dp", axis=1, tiled=True),
    )
    query = jnp.dot(tokens, full_query[0], preferred_element_type=jnp.float32)
    keyval = jnp.dot(tokens, full_keyval[0], preferred_element_type=jnp.float32)
    query = query.astype(jnp.bfloat16).reshape(rollouts, seqlen, width_query)
    keyval = keyval.astype(jnp.bfloat16).reshape(rollouts, seqlen, width_keyval)
    live = lax.dynamic_index_in_dim(lengths, other, 0, keepdims=False)
    attended = jax.vmap(attend)(query, keyval, live)
    return attended[None]


def solution(mesh):
    in_specs = (
        P("pool", "dp", "mp", None),
        P(None, "dp"),
        P(),
        P("pool", ("dp", "mp"), None),
        P("pool", ("dp", "mp"), None),
    )
    out_specs = P("pool", "dp", None, "mp")
    return jax.shard_map(
        on_device, mesh=mesh, in_specs=in_specs, out_specs=out_specs, check_vma=False
    )
```

profile of v0, /device:TPU:0, one launch (start us, length us, event | category | flops | bytes accessed | tf_op | source)
XLA Modules:
  0.0 573.3 jit_solution(5611344158581876059)
XLA Ops:
  6.5 0.0 copy-start
  6.5 0.0 all-gather.4.cloned.1.call-start
  6.5 2.2 fusion.7
  8.7 0.8 dynamic-slice_convert_fusion
  9.5 3.5 fusion.9
  13.1 0.0 all-gather.4.cloned.1.call-update
  13.1 0.0 all-gather.6.cloned.1.call-start
  13.1 0.0 copy-done.2
  13.2 3.0 collective-permute-start.1
  16.2 0.1 collective-permute-start.2
  16.3 23.9 %collective-permute-done.1 = bf16[1,512,1024]{2,1,0:T(8,128)(2,1)S(1)} collective-permute-done((bf16[1,512,1024]{2,1,0:T(8,128)(2,1)S(1)}, bf16[1,512,1024]{2,1,0:T(8,128)(2,1)S(1)}, u32[]{:S(2)}, u32[]{:S(2)}) %collective-permute-start.1) | collective-permute-done | bytes 1048608 | tf_op jit(solution)/shard_map/ppermute | solution.py:13
  40.2 1.8 copy.30
  42.0 0.6 broadcast.68
  42.6 7.3 %reduce.4 = bf16[1024,512]{1,0:T(8,128)(2,1)S(1)} reduce(bf16[1024,1,512]{2,1,0:T(2,128)(2,1)S(1)} %bitcast.94, bf16[]{:T(256)} %broadcast.68), dimensions={1}, to_apply=%bitcast.83.reduce_sub_computation | reduce | bytes 2097154
  49.9 0.8 reshape.124
  50.7 29.2 %all_to_all.36 = bf16[4,2,65536]{2,1,0:T(2,128)(2,1)S(1)} all-to-all(bf16[4,2,65536]{2,1,0:T(2,128)(2,1)S(1)} %reshape.124), channel_id=1, replica_groups=mesh['pool'=2,'dp'=4,'mp'=4] {'mp'}, dimensions={0} | all-to-all | bytes 2097152 | tf_op jit(solution)/shard_map/all_to_all | solution.py:64
  79.9 1.0 reshape.125
  80.9 0.3 copy.41
  81.2 1.3 copy.31
  82.5 0.0 all-gather.6.cloned.1.call-update
  82.5 0.2 all-gather.8.cloned.1.call-start
  82.7 46.6 %collective-permute-done.2 = bf16[1,512,4096]{2,1,0:T(8,128)(2,1)} collective-permute-done((bf16[1,512,4096]{2,1,0:T(8,128)(2,1)}, bf16[1,512,4096]{2,1,0:T(8,128)(2,1)}, u32[]{:S(2)}, u32[]{:S(2)}) %collective-permute-start.2) | collective-permute-done | bytes 4194336 | tf_op jit(solution)/shard_map/ppermute | solution.py:13
  129.3 18.9 %copy.32 = bf16[1,512,4096]{1,0,2:T(2,128)(2,1)} copy(bf16[1,512,4096]{2,1,0:T(8,128)(2,1)} %collective-permute-done.2) | data formatting | bytes 8388608 | tf_op jit(solution)/shard_map/ppermute | solution.py:13
  148.2 28.5 %reduce.3 = bf16[4096,512]{1,0:T(8,128)(2,1)} reduce(bf16[4096,1,512]{2,1,0:T(2,128)(2,1)} %bitcast.89, bf16[]{:T(256)} %broadcast.68), dimensions={1}, to_apply=%bitcast.81.reduce_sub_computation | reduce | bytes 8388610
  176.7 6.2 %reshape.122 = bf16[4,2,262144]{2,1,0:T(2,128)(2,1)} reshape(bf16[4096,512]{1,0:T(8,128)(2,1)} %reduce.3) | data formatting | bytes 8388608
  182.9 53.8 %all_to_all.37 = bf16[4,2,262144]{2,1,0:T(2,128)(2,1)} all-to-all(bf16[4,2,262144]{2,1,0:T(2,128)(2,1)} %reshape.122), channel_id=1, replica_groups=mesh['pool'=2,'dp'=4,'mp'=4] {'mp'}, dimensions={0} | all-to-all | bytes 8388608 | tf_op jit(solution)/shard_map/all_to_all | solution.py:63
  236.8 7.4 %reshape.123 = bf16[4096,1,512]{2,1,0:T(2,128)(2,1)} reshape(bf16[4,2,262144]{2,1,0:T(2,128)(2,1)} %all_to_all.37) | data formatting | bytes 8388608
  244.2 6.6 %copy.42 = bf16[1,512,4096]{1,2,0:T(8,128)(2,1)} copy(bf16[1,512,4096]{1,0,2:T(2,128)(2,1)} %bitcast.90) | data formatting | bytes 8388608
  250.8 6.3 %copy.33 = bf16[1,4,512,1024]{3,2,1,0:T(8,128)(2,1)} copy(bf16[1,4,512,1024]{2,3,1,0:T(8,128)(2,1)} %bitcast.91) | data formatting | bytes 8388608 | tf_op jit(solution)/shard_map/all_to_all | solution.py:63
  257.1 0.0 all-gather.8.cloned.1.call-update
  257.1 0.0 all-gather.4.cloned.1.call-done
  257.2 1.8 collective-permute-start
  259.0 0.0 copy-done
  259.0 0.6 constant_dynamic-slice_fusion
  259.6 0.6 iota_compare_fusion.1
  260.2 0.6 fusion.43
  260.9 0.1 fusion.40
  261.0 0.0 all-gather.6.cloned.1.call-done
  261.0 178.3 %collective-permute-done = bf16[1,1,512,8192]{3,2,1,0:T(8,128)(2,1)} collective-permute-done((bf16[1,1,512,8192]{3,2,1,0:T(8,128)(2,1)}, bf16[1,1,512,8192]{3,2,1,0:T(8,128)(2,1)}, u32[]{:S(2)}, u32[]{:S(2)}) %collective-permute-start) | collective-permute-done | bytes 8388640 | tf_op jit(solution)/shard_map/ppermute | solution.py:13
  439.4 6.9 %fusion.32 = bf16[1,512,1,256]{3,1,2,0:T(8,128)(2,1)S(1)} fusion(bf16[1,8192,256]{2,1,0:T(8,128)(2,1)} %all-gather.6.cloned.1.call-done, bf16[1,1,512,8192]{3,2,1,0:T(8,128)(2,1)} %collective-permute-done), kind=kOutput, calls=%fused_computation.24 | convolution fusion | flops 2147614720 | bytes 12845056 | tf_op jit(solution)/shard_map/dot_general | solution.py:73
  446.3 98.3 %all-gather.8.cloned.1.call-done = bf16[1,8192,1024]{2,1,0:T(8,128)(2,1)} async-done(((bf16[1,2048,1024]{2,1,0:T(8,128)(2,1)}), bf16[1,8192,1024]{2,1,0:T(8,128)(2,1)}) %all-gather.8.cloned.1.call-update) | async-done | bytes 16777232 | tf_op jit(solution)/shard_map/all_gather | solution.py:69
  544.6 14.8 %fusion.22 = bf16[64,8,8,128]{3,2,1,0:T(8,128)(2,1)S(1)} fusion(bf16[1,8192,1024]{2,1,0:T(8,128)(2,1)} %all-gather.8.cloned.1.call-done, bf16[1,1,512,8192]{3,2,1,0:T(8,128)(2,1)} %collective-permute-done), kind=kOutput, calls=%fused_computation.22 | convolution fusion | flops 8590458880 | bytes 26214400 | tf_op jit(solution)/shard_map/dot_general | solution.py:72
  559.4 1.6 fusion.6
  561.0 1.8 fusion.5
  562.8 0.0 copy-start.1
  562.8 2.7 fusion.14
  565.4 1.3 copy.37
  566.8 0.0 copy-done.1
  (2 shorter events, 0.0 us)
Async XLA Ops:
  6.5 252.4 %copy-start = (s32[2,1]{0,1:T(1,128)S(1)}, s32[2,1]{0,1:T(1,128)}, u32[]{:S(2)}) copy-start(s32[2,1]{0,1:T(1,128)} %param.6) | copy-start | bytes 28
  6.5 6.6 %copy-start.2 = (bf16[1,512,1024]{2,1,0:T(8,128)(2,1)S(1)}, bf16[1,512,1024]{2,1,0:T(8,128)(2,1)}, u32[]{:S(2)}) copy-start(bf16[1,512,1024]{2,1,0:T(8,128)(2,1)} %param.9) | copy-start | bytes 3145732
  6.5 250.6 %all-gather.4.cloned.1.call-start = ((), (), s32[]{:S(2)}) async-start(), calls=%async_computation.2 | async-start | bytes 10485760 | tf_op jit(solution)/shard_map/all_gather | solution.py:56
  13.1 247.9 %all-gather.6.cloned.1.call-start = ((), (), s32[]{:S(2)}) async-start(), calls=%async_computation.3 | async-start | bytes 5242880 | tf_op jit(solution)/shard_map/all_gather | solution.py:70
  13.2 27.0 %collective-permute-start.1 = (bf16[1,512,1024]{2,1,0:T(8,128)(2,1)S(1)}, bf16[1,512,1024]{2,1,0:T(8,128)(2,1)S(1)}, u32[]{:S(2)}, u32[]{:S(2)}) collective-permute-start(bf16[1,512,1024]{2,1,0:T(8,128)(2,1)S(1)} %copy-done.2), channel_id=1, source_target_pairs={{0,16},{16,0},{1,17},{17,1},{2,18},{18,2},{3,19},{19,3},{4,20},{20... | collective-permute-start | bytes 3145736 | tf_op jit(solution)/shard_map/ppermute | solution.py:13
  16.2 113.1 %collective-permute-start.2 = (bf16[1,512,4096]{2,1,0:T(8,128)(2,1)}, bf16[1,512,4096]{2,1,0:T(8,128)(2,1)}, u32[]{:S(2)}, u32[]{:S(2)}) collective-permute-start(bf16[1,512,4096]{2,1,0:T(8,128)(2,1)} %param.8), channel_id=1, source_target_pairs={{0,16},{16,0},{1,17},{17,1},{2,18},{18,2},{3,19},{19,3},{4,20},{20... | collective-permute-start | bytes 12582920 | tf_op jit(solution)/shard_map/ppermute | solution.py:13
  82.5 462.1 %all-gather.8.cloned.1.call-start = ((), (), s32[]{:S(2)}) async-start(), calls=%async_computation.4 | async-start | bytes 20971520 | tf_op jit(solution)/shard_map/all_gather | solution.py:69
  257.2 182.2 %collective-permute-start = (bf16[1,1,512,8192]{3,2,1,0:T(8,128)(2,1)}, bf16[1,1,512,8192]{3,2,1,0:T(8,128)(2,1)}, u32[]{:S(2)}, u32[]{:S(2)}) collective-permute-start(bf16[1,1,512,8192]{3,2,1,0:T(8,128)(2,1)} %all-gather.4.cloned.1.call-done), channel_id=1, source_target_pairs={{0,16},{16,0},{1,17},{17,1},{2,18},{18,2},{3,19},{19,3},{4,20},{20... | collective-permute-start | bytes 25165832 | tf_op jit(solution)/shard_map/ppermute | solution.py:13
  562.8 4.0 copy-start.1
Sparse Core Ops, SparseCore 0:
  13.2 72.2 all-gather.3
  87.0 80.7 all-gather.5
  257.3 287.2 all-gather.7
where the time goes:
time: 575 us; the launch traced here: 573 us
  waiting for transfers between devices  347 us (60%)
  blocking collectives  83 us (14%)
  local copies, waits for them, and re-layouts  53.2 us (9%)
  other arithmetic  45.4 us (8%)
  matrix products  26 us (5%)
  between operations  13.2 us (2%)
    ppermute x3, waiting for transfers between devices, partner(): lax.ppermute(value, axis, [(i, i ^ 1 << distance) for i in range(lax.axis...  249 us
    all_gather x1, waiting for transfers between devices, on_device(): lax.all_gather(query_cols, 'dp', axis=1, tiled=True)  98.3 us
    all_to_all x1, blocking collectives, on_device(): lax.all_to_all(rows_query, 'mp', split_axis=2, concat_axis=1, tiled=True)  53.8 us
    unnamed x2, other arithmetic  35.7 us
    all_to_all x1, blocking collectives, on_device(): lax.all_to_all(rows_keyval, 'mp', split_axis=2, concat_axis=1, tiled=True)  29.2 us
    unnamed x13, local copies, waits for them, and re-layouts  22.9 us
    ppermute x2, local copies, waits for them, and re-layouts, partner(): lax.ppermute(value, axis, [(i, i ^ 1 << distance) for i in range(lax.axis...  20.7 us
    dot_general x1, matrix products, on_device(): query = jnp.dot(tokens, full_query[0], preferred_element_type=jnp.float32)  14.8 us
  transfers between devices with their start and end apart: 6, of which 4 were waited for; matrix products, arithmetic and copies ran while one was open for 17% of the time, Pallas kernels for 0%

commit v1 on v0

--- a/solution.py
+++ b/solution.py
@@ -7,6 +7,13 @@
 HD = 128
 QH = 32
 KVH = 4
+
+
+def swap_blocks(x, axis, split, join):
+    size = lax.axis_size(axis)
+    pieces = jnp.stack(jnp.split(x, size, axis=split), axis=0)
+    pieces = lax.all_to_all(pieces, axis, split_axis=0, concat_axis=0)
+    return jnp.concatenate(pieces, axis=join)
 
 
 def partner(value, axis, distance):
@@ -60,7 +67,7 @@
     tokens = whole[0].reshape(rollouts * seqlen, whole.shape[3])
     rows_query, rows_keyval = partner((w_query, w_keyval), "pool", 0)
     query_cols, keyval_cols = (
-        lax.all_to_all(rows_query, "mp", split_axis=2, concat_axis=1, tiled=True),
+        swap_blocks(rows_query, "mp", 2, 1),
         lax.all_to_all(rows_keyval, "mp", split_axis=2, concat_axis=1, tiled=True),
     )
     width_query = query_cols.shape[2]

time: 575 us -> 501 us (0.87)
  local copies, waits for them, and re-layouts: 53.2 us -> 10.3 us
  other arithmetic: 45.4 us -> 17.5 us
    unnamed x2 -> x1, other arithmetic: 35.7 us -> 7.31 us
    unnamed x13 -> x10, local copies, waits for them, and re-layouts: 22.9 us -> 2.56 us
    ppermute x2 -> x1, local copies, waits for them, and re-layouts: 20.7 us -> 1.82 us  [partner(): lax.ppermute(value, axis, [(i, i ^ 1 << distance) for i in range(lax.axis...]
    all_to_all x1 -> x0, local copies, waits for them, and re-layouts: 6.34 us -> none  [on_device(): lax.all_to_all(rows_query, 'mp', split_axis=2, concat_axis=1, tiled=True)]
  transfers between devices with their start and end apart: 6 -> 6, of which waited for: 4 -> 4; matrix products, arithmetic and copies ran while one was open for 17% -> 5% of each run, Pallas kernels for 0% -> 0%
where the time goes in v1:
time: 501 us; the launch traced here: 500 us
  waiting for transfers between devices  347 us (69%)
  blocking collectives  80.8 us (16%)
  matrix products  26 us (5%)
  other arithmetic  17.5 us (3%)
  between operations  13.2 us (3%)
  local copies, waits for them, and re-layouts  10.3 us (2%)
    ppermute x3, waiting for transfers between devices, partner(): lax.ppermute(value, axis, [(i, i ^ 1 << distance) for i in range(lax.axis...  249 us
    all_gather x1, waiting for transfers between devices, on_device(): lax.all_gather(query_cols, 'dp', axis=1, tiled=True)  98.2 us
    all_to_all x1, blocking collectives, swap_blocks(): pieces = lax.all_to_all(pieces, axis, split_axis=0, concat_axis=0)  51.5 us
    all_to_all x1, blocking collectives, on_device(): lax.all_to_all(rows_keyval, 'mp', split_axis=2, concat_axis=1, tiled=True)  29.2 us
    dot_general x1, matrix products, on_device(): query = jnp.dot(tokens, full_query[0], preferred_element_type=jnp.float32)  14.8 us
  transfers between devices with their start and end apart: 6, of which 4 were waited for; matrix products, arithmetic and copies ran while one was open for 5% of the time, Pallas kernels for 0%

profile of v1, /device:TPU:0, one launch (start us, length us, event | category | flops | bytes accessed | tf_op | source)
XLA Modules:
  0.0 500.2 jit_solution(4993964522386417077)
XLA Ops:
  6.5 0.0 copy-start
  6.5 0.0 all-gather.4.cloned.1.call-start
  6.5 0.0 copy-start.2
  6.5 2.2 fusion.7
  8.7 0.8 dynamic-slice_convert_fusion
  9.5 3.5 fusion.9
  13.0 0.0 all-gather.4.cloned.1.call-update
  13.1 0.0 all-gather.6.cloned.1.call-start
  13.1 0.0 copy-done.2
  13.1 3.0 collective-permute-start.1
  16.1 0.1 collective-permute-start.2
  16.2 23.9 %collective-permute-done.1 = bf16[1,512,1024]{2,1,0:T(8,128)(2,1)S(1)} collective-permute-done((bf16[1,512,1024]{2,1,0:T(8,128)(2,1)S(1)}, bf16[1,512,1024]{2,1,0:T(8,128)(2,1)S(1)}, u32[]{:S(2)}, u32[]{:S(2)}) %collective-permute-start.1) | collective-permute-done | bytes 1048608 | tf_op jit(solution)/shard_map/ppermute | solution.py:20
  40.2 1.8 copy.26
  42.0 0.5 broadcast.68
  42.5 7.3 %reduce.3 = bf16[1024,512]{1,0:T(8,128)(2,1)S(1)} reduce(bf16[1024,1,512]{2,1,0:T(2,128)(2,1)S(1)} %bitcast.94, bf16[]{:T(256)} %broadcast.68), dimensions={1}, to_apply=%bitcast.86.reduce_sub_computation | reduce | bytes 2097154
  49.8 0.8 reshape.126
  50.6 29.2 %all_to_all.23 = bf16[4,2,65536]{2,1,0:T(2,128)(2,1)S(1)} all-to-all(bf16[4,2,65536]{2,1,0:T(2,128)(2,1)S(1)} %reshape.126), channel_id=1, replica_groups=mesh['pool'=2,'dp'=4,'mp'=4] {'mp'}, dimensions={0} | all-to-all | bytes 2097152 | tf_op jit(solution)/shard_map/all_to_all | solution.py:71
  79.8 1.0 reshape.127
  80.8 0.3 copy.35
  81.1 1.3 copy.27
  82.4 0.0 all-gather.6.cloned.1.call-update
  82.4 0.0 all-gather.8.cloned.1.call-start
  82.5 46.8 %collective-permute-done.2 = bf16[1,512,4096]{2,1,0:T(8,128)(2,1)} collective-permute-done((bf16[1,512,4096]{2,1,0:T(8,128)(2,1)}, bf16[1,512,4096]{2,1,0:T(8,128)(2,1)}, u32[]{:S(2)}, u32[]{:S(2)}) %collective-permute-start.2) | collective-permute-done | bytes 4194336 | tf_op jit(solution)/shard_map/ppermute | solution.py:20
  129.3 2.7 slice_bitcast_fusion.3
  132.0 0.6 pad_maximum_fusion
  132.6 51.5 %all_to_all.24 = bf16[4,1,512,1024]{3,2,1,0:T(8,128)(2,1)} all-to-all(bf16[4,1,512,1024]{3,2,1,0:T(8,128)(2,1)S(1)} %pad_maximum_fusion), channel_id=1, replica_groups=mesh['pool'=2,'dp'=4,'mp'=4] {'mp'}, dimensions={0} | all-to-all | bytes 8388608 | tf_op jit(solution)/shard_map/all_to_all | solution.py:15
  184.1 0.0 all-gather.8.cloned.1.call-update
  184.1 0.0 all-gather.4.cloned.1.call-done
  184.2 1.8 collective-permute-start
  186.0 0.0 copy-done
  186.0 0.6 constant_dynamic-slice_fusion
  186.6 0.6 iota_compare_fusion.1
  187.2 0.6 fusion.43
  187.9 0.1 fusion.40
  188.0 0.0 all-gather.6.cloned.1.call-done
  188.0 178.3 %collective-permute-done = bf16[1,1,512,8192]{3,2,1,0:T(8,128)(2,1)} collective-permute-done((bf16[1,1,512,8192]{3,2,1,0:T(8,128)(2,1)}, bf16[1,1,512,8192]{3,2,1,0:T(8,128)(2,1)}, u32[]{:S(2)}, u32[]{:S(2)}) %collective-permute-start) | collective-permute-done | bytes 8388640 | tf_op jit(solution)/shard_map/ppermute | solution.py:20
  366.4 6.9 %fusion.32 = bf16[1,512,1,256]{3,1,2,0:T(8,128)(2,1)S(1)} fusion(bf16[1,8192,256]{2,1,0:T(8,128)(2,1)} %all-gather.6.cloned.1.call-done, bf16[1,1,512,8192]{3,2,1,0:T(8,128)(2,1)} %collective-permute-done), kind=kOutput, calls=%fused_computation.25 | convolution fusion | flops 2147614720 | bytes 12845056 | tf_op jit(solution)/shard_map/dot_general | solution.py:80
  373.3 98.2 %all-gather.8.cloned.1.call-done = bf16[1,8192,1024]{2,1,0:T(8,128)(2,1)} async-done(((bf16[1,2048,1024]{2,1,0:T(8,128)(2,1)}), bf16[1,8192,1024]{2,1,0:T(8,128)(2,1)}) %all-gather.8.cloned.1.call-update) | async-done | bytes 16777232 | tf_op jit(solution)/shard_map/all_gather | solution.py:76
  471.5 14.8 %fusion.22 = bf16[64,8,8,128]{3,2,1,0:T(8,128)(2,1)S(1)} fusion(bf16[1,8192,1024]{2,1,0:T(8,128)(2,1)} %all-gather.8.cloned.1.call-done, bf16[1,1,512,8192]{3,2,1,0:T(8,128)(2,1)} %collective-permute-done), kind=kOutput, calls=%fused_computation.23 | convolution fusion | flops 8590458880 | bytes 26214400 | tf_op jit(solution)/shard_map/dot_general | solution.py:79
  486.3 1.6 fusion.6
  488.0 1.7 fusion.5
  489.7 0.0 copy-start.1
  489.7 2.7 fusion.14
  492.4 1.3 copy.31
  493.7 0.0 copy-done.1
  (1 shorter events, 0.0 us)
Async XLA Ops:
  6.5 179.4 %copy-start = (s32[2,1]{0,1:T(1,128)S(1)}, s32[2,1]{0,1:T(1,128)}, u32[]{:S(2)}) copy-start(s32[2,1]{0,1:T(1,128)} %param.6) | copy-start | bytes 28
  6.5 177.6 %all-gather.4.cloned.1.call-start = ((), (), s32[]{:S(2)}) async-start(), calls=%async_computation.2 | async-start | bytes 10485760 | tf_op jit(solution)/shard_map/all_gather | solution.py:63
  6.5 6.6 %copy-start.2 = (bf16[1,512,1024]{2,1,0:T(8,128)(2,1)S(1)}, bf16[1,512,1024]{2,1,0:T(8,128)(2,1)}, u32[]{:S(2)}) copy-start(bf16[1,512,1024]{2,1,0:T(8,128)(2,1)} %param.9) | copy-start | bytes 3145732
  13.1 175.0 %all-gather.6.cloned.1.call-start = ((), (), s32[]{:S(2)}) async-start(), calls=%async_computation.3 | async-start | bytes 5242880 | tf_op jit(solution)/shard_map/all_gather | solution.py:77
  13.1 27.0 %collective-permute-start.1 = (bf16[1,512,1024]{2,1,0:T(8,128)(2,1)S(1)}, bf16[1,512,1024]{2,1,0:T(8,128)(2,1)S(1)}, u32[]{:S(2)}, u32[]{:S(2)}) collective-permute-start(bf16[1,512,1024]{2,1,0:T(8,128)(2,1)S(1)} %copy-done.2), channel_id=1, source_target_pairs={{0,16},{16,0},{1,17},{17,1},{2,18},{18,2},{3,19},{19,3},{4,20},{20... | collective-permute-start | bytes 3145736 | tf_op jit(solution)/shard_map/ppermute | solution.py:20
  16.1 113.1 %collective-permute-start.2 = (bf16[1,512,4096]{2,1,0:T(8,128)(2,1)}, bf16[1,512,4096]{2,1,0:T(8,128)(2,1)}, u32[]{:S(2)}, u32[]{:S(2)}) collective-permute-start(bf16[1,512,4096]{2,1,0:T(8,128)(2,1)} %param.8), channel_id=1, source_target_pairs={{0,16},{16,0},{1,17},{17,1},{2,18},{18,2},{3,19},{19,3},{4,20},{20... | collective-permute-start | bytes 12582920 | tf_op jit(solution)/shard_map/ppermute | solution.py:20
  82.4 389.1 %all-gather.8.cloned.1.call-start = ((), (), s32[]{:S(2)}) async-start(), calls=%async_computation.4 | async-start | bytes 20971520 | tf_op jit(solution)/shard_map/all_gather | solution.py:76
  184.2 182.2 %collective-permute-start = (bf16[1,1,512,8192]{3,2,1,0:T(8,128)(2,1)}, bf16[1,1,512,8192]{3,2,1,0:T(8,128)(2,1)}, u32[]{:S(2)}, u32[]{:S(2)}) collective-permute-start(bf16[1,1,512,8192]{3,2,1,0:T(8,128)(2,1)} %all-gather.4.cloned.1.call-done), channel_id=1, source_target_pairs={{0,16},{16,0},{1,17},{17,1},{2,18},{18,2},{3,19},{19,3},{4,20},{20... | collective-permute-start | bytes 25165832 | tf_op jit(solution)/shard_map/ppermute | solution.py:20
  489.7 4.0 copy-start.1
Sparse Core Ops, SparseCore 0:
  13.2 72.2 all-gather.3
  87.0 80.7 all-gather.5
  184.3 287.2 all-gather.7
